TPU v7x, 32 devices: a whole 2x2x4 slice. The times are simulated.
32 devices in a mesh: member: 16 (over z, y, core), slab: 2 (over x).
Axes of the slice: x: 2, y: 2, z: 4, core: 2. Of those that a mesh axis runs over, the one named last changes fastest.
Arguments:
- checkpoint: float32 [16, 2, 4, 256, 256], P('member', None, 'slab'), may hold values from 0 to 1
- adjoint_late: float32 [16, 2, 4, 256, 256], P('member', None, 'slab'), may hold values from -6 to 6
- rate_params: float32 [64, 64], replicated, may hold values from 0.02 to 0.1
- perturbation: float32 [16, 64, 64], P('member'), may hold values from -0.5 to 0.5
Outputs:
- adjoint_early: float32 [16, 2, 4, 256, 256], P('member', None, 'slab')
- param_grad: float32 [64, 64], replicated
All inputs are finite; a program needn't handle non-finite values.
Results may differ from a plain program's by a relative error of at most 0.00002.
Values sent between devices are 32-bit elements; how exact they have to be, the bound alone decides.
No kernel may reach another device: no remote copies, remote signals or barrier semaphores. Data moves between devices by JAX's collectives and lax.ppermute only.
A program may use at most 64 MiB of HBM per device.

v0:
```python
import jax
import jax.numpy as jnp
from jax import lax
from jax.sharding import PartitionSpec as P

PX = 64
PY = 64
SX = 4
SY = 4
NX = 256
NY = 256


feed_rate = 0.035
substrate_diffusion = 0.16
activator_diffusion = 0.08


def with_halo(cells, sides, width):
    for axis, dim in sides:
        count = lax.axis_size(axis)
        ends = count - 1
        head = lax.slice_in_dim(cells, 0, width, axis=dim)
        tail = lax.slice_in_dim(cells, cells.shape[dim] - width, cells.shape[dim], axis=dim)
        cells = jnp.concatenate(
            [
                lax.ppermute(tail, axis, [(i, (i + 1) % count) for i in range(ends)]),
                cells,
                lax.ppermute(head, axis, [((i + 1) % count, i) for i in range(ends)]),
            ],
            axis=dim,
        )
    return cells


def laplace_rim(extended):
    padded = jnp.pad(extended, ((0, 0), (0, 0), (1, 1), (1, 1)))
    center = padded[:, 1:-1, 1:-1, 1:-1]
    summed = padded[:, 2:, 1:-1, 1:-1] + padded[:, :-2, 1:-1, 1:-1]
    summed = summed + padded[:, 1:-1, 2:, 1:-1] + padded[:, 1:-1, :-2, 1:-1]
    summed = summed + padded[:, 1:-1, 1:-1, 2:] + padded[:, 1:-1, 1:-1, :-2]
    return summed - 6.0 * center


def advance(extended, decay_rate):
    laplace = laplace_rim(extended)
    u_field = extended[0, 1:-1]
    v_field = extended[1, 1:-1]
    reaction = u_field * v_field * v_field
    u_new = u_field + substrate_diffusion * laplace[0] - reaction + feed_rate * (1.0 - u_field)
    v_new = (
        v_field + activator_diffusion * laplace[1] + reaction - (feed_rate + decay_rate) * v_field
    )
    return jnp.stack([u_new, v_new])


def pull_back(status, adjoint_ext, decay_rate):
    laplace = laplace_rim(adjoint_ext)
    adj_u = adjoint_ext[0, 1:-1]
    adj_v = adjoint_ext[1, 1:-1]
    uv_prod = status[0] * status[1]
    v_square = status[1] * status[1]
    new_u = (
        adj_u + substrate_diffusion * laplace[0] - (v_square + feed_rate) * adj_u + v_square * adj_v
    )
    new_v = (
        adj_v
        + activator_diffusion * laplace[1]
        - 2.0 * uv_prod * adj_u
        + (2.0 * uv_prod - feed_rate - decay_rate) * adj_v
    )
    return jnp.stack([new_u, new_v])


def expand_params(table):
    return jnp.broadcast_to(table[:, None, :, None], (PX, SX, PY, SY)).reshape(NX, NY)


def patch_total(field):
    return jnp.sum(field.reshape(PX, SX, PY, SY), axis=(1, 3))


def local(checkpoint, adjoint_late, rate_params, perturbation):
    start_state = checkpoint[0]
    adjoint_two = adjoint_late[0]
    factor = 1.0 + perturbation[0]
    decay_rate = expand_params(rate_params * factor)
    member_count = lax.axis_size("member")
    state_ext, adjoint_ext_two = (
        with_halo(start_state, (("slab", 1),), 1),
        with_halo(adjoint_two, (("slab", 1),), 1),
    )
    middle = advance(state_ext, decay_rate)
    adjoint_one = pull_back(middle, adjoint_ext_two, decay_rate)
    first_term = -jnp.sum(middle[1] * adjoint_two[1], 0)
    adjoint_ext = with_halo(adjoint_one, (("slab", 1),), 1)
    adjoint_zero = pull_back(start_state, adjoint_ext, decay_rate)
    second = -jnp.sum(start_state[1] * adjoint_one[1], 0)
    param_grad = (
        lax.psum(patch_total(first_term + second) * factor, ("member", "slab")) / member_count
    )
    return (adjoint_zero[None], param_grad)


def solution(mesh):
    return jax.shard_map(
        local,
        mesh=mesh,
        in_specs=(
            P("member", None, "slab", None, None),
            P("member", None, "slab", None, None),
            P(),
            P("member", None, None),
        ),
        out_specs=(P("member", None, "slab", None, None), P()),
        check_vma=False,
    )
```

profile of v0, /device:TPU:0, one launch (start us, length us, event | category | flops | bytes accessed | tf_op | source)
XLA Modules:
  0.0 109.7 jit_solution(6081477376851431871)
XLA Ops:
  0.6 0.0 copy-start.5
  0.6 0.0 copy-start.4
  0.6 2.3 %fusion.44 = (f32[2,1,256,256]{3,2,1,0:T(8,128)}, f32[2,1,256,256]{3,2,1,0:T(8,128)}) fusion(f32[2,2,256,256]{3,2,1,0:T(8,128)} %bitcast.149), kind=kLoop, calls=%fused_computation.112 | loop fusion | bytes 2097152 | tf_op jit(solution)/shard_map/slice | solution.py:24
  2.9 1.3 %collective-permute-start = (f32[2,1,256,256]{3,2,1,0:T(8,128)}, f32[2,1,256,256]{3,2,1,0:T(8,128)S(1)}, u32[]{:S(2)}, u32[]{:S(2)}) collective-permute-start(f32[2,1,256,256]{3,2,1,0:T(8,128)} %get-tuple-element.13), channel_id=1, source_target_pairs={{1,0},{3,2},{5,4},{7,6},{9,8},{11,10},{13,12},{15,14},{17,16},{19,... | collective-permute-start | bytes 1572872 | tf_op jit(solution)/shard_map/ppermute | solution.py:29
  4.2 4.9 %collective-permute-start.1 = (f32[2,1,256,256]{3,2,1,0:T(8,128)}, f32[2,1,256,256]{3,2,1,0:T(8,128)S(1)}, u32[]{:S(2)}, u32[]{:S(2)}) collective-permute-start(f32[2,1,256,256]{3,2,1,0:T(8,128)} %get-tuple-element.12), channel_id=1, source_target_pairs={{0,1},{2,3},{4,5},{6,7},{8,9},{10,11},{12,13},{14,15},{16,17},{18,... | collective-permute-start | bytes 1572872 | tf_op jit(solution)/shard_map/ppermute | solution.py:27
  9.1 2.4 %fusion.43 = (f32[2,1,256,256]{3,2,1,0:T(8,128)}, f32[2,1,256,256]{3,2,1,0:T(8,128)}) fusion(f32[2,2,256,256]{3,2,1,0:T(8,128)} %bitcast.146), kind=kLoop, calls=%fused_computation.111 | loop fusion | bytes 2097152 | tf_op jit(solution)/shard_map/slice | solution.py:24
  11.5 1.3 %collective-permute-start.2 = (f32[2,1,256,256]{3,2,1,0:T(8,128)}, f32[2,1,256,256]{3,2,1,0:T(8,128)S(1)}, u32[]{:S(2)}, u32[]{:S(2)}) collective-permute-start(f32[2,1,256,256]{3,2,1,0:T(8,128)} %get-tuple-element.11), channel_id=1, source_target_pairs={{1,0},{3,2},{5,4},{7,6},{9,8},{11,10},{13,12},{15,14},{17,16},{19,... | collective-permute-start | bytes 1572872 | tf_op jit(solution)/shard_map/ppermute | solution.py:29
  12.8 5.4 %collective-permute-start.3 = (f32[2,1,256,256]{3,2,1,0:T(8,128)}, f32[2,1,256,256]{3,2,1,0:T(8,128)}, u32[]{:S(2)}, u32[]{:S(2)}) collective-permute-start(f32[2,1,256,256]{3,2,1,0:T(8,128)} %get-tuple-element.10), channel_id=1, source_target_pairs={{0,1},{2,3},{4,5},{6,7},{8,9},{10,11},{12,13},{14,15},{16,17},{18,... | collective-permute-start | bytes 1572872 | tf_op jit(solution)/shard_map/ppermute | solution.py:27
  18.2 0.0 copy-done.5
  18.2 0.0 copy-done.4
  18.2 3.8 %broadcast_in_dim.4 = f32[64,4,64,4]{3,2,1,0:T(8,128)} broadcast(f32[64,64]{1,0:T(8,128)S(1)} %bitcast_multiply_fusion.13), dimensions={0,2} | broadcast | bytes 278528 | tf_op jit(solution)/shard_map/broadcast_in_dim | solution.py:76
  22.0 0.0 copy-start.1
  22.0 8.4 %reshape.133 = f32[256,256]{1,0:T(8,128)S(1)} reshape(f32[64,4,64,4]{3,2,1,0:T(8,128)} %broadcast_in_dim.4) | data formatting | bytes 524288 | tf_op jit(solution)/shard_map/reshape | solution.py:76
  30.4 0.0 collective-permute-done
  30.4 0.0 copy-start.2
  30.4 0.0 collective-permute-done.1
  30.5 0.8 copy-done.2
  31.2 0.0 copy-start.3
  31.2 0.8 copy-done.3
  32.0 0.0 copy-done.1
  32.0 1.4 %select_maximum_fusion.5 = f32[2,4,258,258]{3,2,1,0:T(8,128)S(1)} fusion(f32[2,1,256,256]{3,2,1,0:T(8,128)S(1)} %collective-permute-done, f32[2,2,256,256]{3,2,1,0:T(8,128)S(1)} %bitcast.150, f32[2,1,256,256]{3,2,1,0:T(8,128)S(1)} %collective-permute-done.1), kind=kLoop, calls=%fused_computation.9 | loop fusion | flops 7987680 | bytes 4227200 | tf_op jit(solution)/shard_map/concatenate | solution.py:25
  33.5 0.0 copy-start
  33.5 2.2 %fusion.8 = f32[2,2,256,256]{3,2,1,0:T(8,128)S(1)} fusion(f32[2,4,258,258]{3,2,1,0:T(8,128)S(1)} %select_maximum_fusion.5, f32[2,2,256,256]{3,2,1,0:T(8,128)S(1)} %bitcast.151, f32[2,1,256,256]{3,2,1,0:T(8,128)} %copy-done.3, f32[2,1,256,256]{3,2,1,0:T(8,128)} %copy-done.2), kind=kLoop, calls=%fused_computation.39 | loop fusion | flops 2359296 | bytes 7340032 | tf_op jit(solution)/shard_map/sub | solution.py:42
  35.7 0.0 collective-permute-done.2
  35.7 0.0 collective-permute-done.3
  35.7 0.0 copy-done
  35.7 2.4 %select_maximum_fusion.3 = f32[2,4,258,258]{3,2,1,0:T(8,128)S(1)} fusion(f32[2,1,256,256]{3,2,1,0:T(8,128)S(1)} %collective-permute-done.2, f32[2,2,256,256]{3,2,1,0:T(8,128)S(1)} %bitcast.147, f32[2,1,256,256]{3,2,1,0:T(8,128)} %collective-permute-done.3), kind=kLoop, calls=%fused_computation.7 | loop fusion | flops 7987680 | bytes 4227200 | tf_op jit(solution)/shard_map/concatenate | solution.py:25
  38.2 2.0 %fusion.6 = f32[2,2,256,256]{3,2,1,0:T(8,128)S(1)} fusion(f32[2,4,258,258]{3,2,1,0:T(8,128)S(1)} %select_maximum_fusion.3, f32[2,2,256,256]{3,2,1,0:T(8,128)S(1)} %bitcast.148, f32[2,1,256,256]{3,2,1,0:T(8,128)} %collective-permute-done.3, f32[2,1,256,256]{3,2,1,0:T(8,128)S(1)} %collective-permute-done.2), kind=kLoop, calls=%fused_computation.31 | loop fusion | flops 2359296 | bytes 7340032 | tf_op jit(solution)/shard_map/sub | solution.py:42
  40.2 0.3 fusion.20
  40.4 0.5 fusion.29
  40.9 0.4 fusion.34
  41.3 1.1 fusion.11
  42.4 1.3 %collective-permute-start.4 = (f32[2,1,256,256]{3,2,1,0:T(8,128)}, f32[2,1,256,256]{3,2,1,0:T(8,128)S(1)}, u32[]{:S(2)}, u32[]{:S(2)}) collective-permute-start(f32[2,1,256,256]{3,2,1,0:T(8,128)} %get-tuple-element.9), channel_id=1, source_target_pairs={{1,0},{3,2},{5,4},{7,6},{9,8},{11,10},{13,12},{15,14},{17,16},{19,... | collective-permute-start | bytes 1572872 | tf_op jit(solution)/shard_map/ppermute | solution.py:29
  43.7 4.6 %collective-permute-start.5 = (f32[2,1,256,256]{3,2,1,0:T(8,128)}, f32[2,1,256,256]{3,2,1,0:T(8,128)S(1)}, u32[]{:S(2)}, u32[]{:S(2)}) collective-permute-start(f32[2,1,256,256]{3,2,1,0:T(8,128)} %get-tuple-element.8), channel_id=1, source_target_pairs={{0,1},{2,3},{4,5},{6,7},{8,9},{10,11},{12,13},{14,15},{16,17},{18,... | collective-permute-start | bytes 1572872 | tf_op jit(solution)/shard_map/ppermute | solution.py:27
  48.3 0.8 negate_add_fusion
  49.0 10.8 %add.226 = f32[64,4,64,4]{3,2,1,0:T(8,128)} reshape(f32[256,256]{1,0:T(8,128)} %negate_add_fusion) | data formatting | bytes 524288 | tf_op jit(solution)/shard_map/add | solution.py:100
  59.9 4.0 %reduce_sum.29 = f32[64,64]{1,0:T(8,128)S(1)} reduce(f32[64,4,64,4]{3,2,1,0:T(8,128)} %add.226, f32[]{:T(128)} %constant.9.clone.1), dimensions={1,3}, to_apply=%region_2.3 | reduce | flops 61440 | bytes 278532 | tf_op jit(solution)/shard_map/reduce_sum | solution.py:80
  63.9 41.0 %psum.7 = f32[64,64]{1,0:T(8,128)S(1)} all-reduce(f32[64,64]{1,0:T(8,128)S(1)} %bitcast_multiply_fusion.12), channel_id=1, replica_groups=mesh['member'=16,'slab'=2] {'member','slab'}, use_global_device_ids=true, to_apply=%region_3.4 | all-reduce | flops 4096 | bytes 32768 | tf_op jit(solution)/shard_map/psum | solution.py:100
  104.9 0.6 broadcast_multiply_fusion
  105.5 0.0 collective-permute-done.4
  105.5 0.0 collective-permute-done.5
  105.5 1.9 %select_maximum_fusion = f32[2,4,258,258]{3,2,1,0:T(8,128)S(1)} fusion(f32[2,1,256,256]{3,2,1,0:T(8,128)S(1)} %collective-permute-done.4, f32[2,1,256,256]{3,2,1,0:T(8,128)S(1)} %collective-permute-done.5, f32[1,2,256,256]{3,2,1,0:T(8,128)S(1)} %fusion.34, f32[1,2,256,256]{3,2,1,0:T(8,128)S(1)} %get-tuple-element.4), kind=kLoop, calls=%fused_computation.4 | loop fusion | flops 9585216 | bytes 4227200 | tf_op jit(solution)/shard_map/concatenate | solution.py:25
  107.4 0.9 fusion.4
  108.4 0.3 fusion.17
  108.7 1.0 maximum_bitcast_fusion
  (3 shorter events, 0.0 us)
Async XLA Ops:
  0.6 17.5 %copy-start.5 = (f32[64,64]{1,0:T(8,128)S(1)}, f32[64,64]{1,0:T(8,128)}, u32[]{:S(2)}) copy-start(f32[64,64]{1,0:T(8,128)} %param.6) | copy-start | bytes 49156
  0.6 17.5 %copy-start.4 = (f32[1,64,64]{2,1,0:T(8,128)S(1)}, f32[1,64,64]{2,1,0:T(8,128)}, u32[]{:S(2)}) copy-start(f32[1,64,64]{2,1,0:T(8,128)} %param.7) | copy-start | bytes 49156
  2.9 27.5 %collective-permute-start = (f32[2,1,256,256]{3,2,1,0:T(8,128)}, f32[2,1,256,256]{3,2,1,0:T(8,128)S(1)}, u32[]{:S(2)}, u32[]{:S(2)}) collective-permute-start(f32[2,1,256,256]{3,2,1,0:T(8,128)} %get-tuple-element.13), channel_id=1, source_target_pairs={{1,0},{3,2},{5,4},{7,6},{9,8},{11,10},{13,12},{15,14},{17,16},{19,... | collective-permute-start | bytes 1572872 | tf_op jit(solution)/shard_map/ppermute | solution.py:29
  4.2 26.3 %collective-permute-start.1 = (f32[2,1,256,256]{3,2,1,0:T(8,128)}, f32[2,1,256,256]{3,2,1,0:T(8,128)S(1)}, u32[]{:S(2)}, u32[]{:S(2)}) collective-permute-start(f32[2,1,256,256]{3,2,1,0:T(8,128)} %get-tuple-element.12), channel_id=1, source_target_pairs={{0,1},{2,3},{4,5},{6,7},{8,9},{10,11},{12,13},{14,15},{16,17},{18,... | collective-permute-start | bytes 1572872 | tf_op jit(solution)/shard_map/ppermute | solution.py:27
  11.5 24.2 %collective-permute-start.2 = (f32[2,1,256,256]{3,2,1,0:T(8,128)}, f32[2,1,256,256]{3,2,1,0:T(8,128)S(1)}, u32[]{:S(2)}, u32[]{:S(2)}) collective-permute-start(f32[2,1,256,256]{3,2,1,0:T(8,128)} %get-tuple-element.11), channel_id=1, source_target_pairs={{1,0},{3,2},{5,4},{7,6},{9,8},{11,10},{13,12},{15,14},{17,16},{19,... | collective-permute-start | bytes 1572872 | tf_op jit(solution)/shard_map/ppermute | solution.py:29
  12.8 23.0 %collective-permute-start.3 = (f32[2,1,256,256]{3,2,1,0:T(8,128)}, f32[2,1,256,256]{3,2,1,0:T(8,128)}, u32[]{:S(2)}, u32[]{:S(2)}) collective-permute-start(f32[2,1,256,256]{3,2,1,0:T(8,128)} %get-tuple-element.10), channel_id=1, source_target_pairs={{0,1},{2,3},{4,5},{6,7},{8,9},{10,11},{12,13},{14,15},{16,17},{18,... | collective-permute-start | bytes 1572872 | tf_op jit(solution)/shard_map/ppermute | solution.py:27
  22.0 10.0 %copy-start.1 = (f32[1,2,2,256,256]{4,3,2,1,0:T(8,128)S(1)}, f32[1,2,2,256,256]{4,3,2,1,0:T(8,128)}, u32[]{:S(2)}) copy-start(f32[1,2,2,256,256]{4,3,2,1,0:T(8,128)} %param.5) | copy-start | bytes 3145732
  30.4 0.8 copy-start.2
  31.2 0.8 copy-start.3
  33.5 2.3 %copy-start = (f32[1,2,2,256,256]{4,3,2,1,0:T(8,128)S(1)}, f32[1,2,2,256,256]{4,3,2,1,0:T(8,128)}, u32[]{:S(2)}) copy-start(f32[1,2,2,256,256]{4,3,2,1,0:T(8,128)} %param.4) | copy-start | bytes 3145732
  42.4 63.2 %collective-permute-start.4 = (f32[2,1,256,256]{3,2,1,0:T(8,128)}, f32[2,1,256,256]{3,2,1,0:T(8,128)S(1)}, u32[]{:S(2)}, u32[]{:S(2)}) collective-permute-start(f32[2,1,256,256]{3,2,1,0:T(8,128)} %get-tuple-element.9), channel_id=1, source_target_pairs={{1,0},{3,2},{5,4},{7,6},{9,8},{11,10},{13,12},{15,14},{17,16},{19,... | collective-permute-start | bytes 1572872 | tf_op jit(solution)/shard_map/ppermute | solution.py:29
  43.7 61.9 %collective-permute-start.5 = (f32[2,1,256,256]{3,2,1,0:T(8,128)}, f32[2,1,256,256]{3,2,1,0:T(8,128)S(1)}, u32[]{:S(2)}, u32[]{:S(2)}) collective-permute-start(f32[2,1,256,256]{3,2,1,0:T(8,128)} %get-tuple-element.8), channel_id=1, source_target_pairs={{0,1},{2,3},{4,5},{6,7},{8,9},{10,11},{12,13},{14,15},{16,17},{18,... | collective-permute-start | bytes 1572872 | tf_op jit(solution)/shard_map/ppermute | solution.py:27
where the time goes:
time: 110 us
  blocking collectives  41 us (37%)
  local copies, waits for them, and re-layouts  29.3 us (27%)
  other arithmetic  19.8 us (18%)
  starting transfers between devices  18.8 us (17%)
    psum x1, blocking collectives, local(): lax.psum(patch_total(first_term + second) * factor, ('member', 'slab'))  41 us
    ppermute x3, starting transfers between devices, with_halo(): lax.ppermute(tail, axis, [(i, (i + 1) % count) for i in range(ends)])  14.9 us
    add x1, local copies, waits for them, and re-layouts, local(): first_term + second  10.8 us
    reshape x1, local copies, waits for them, and re-layouts, expand_params(): jnp.broadcast_to(table[:, None, :, None], (PX, SX, PY, SY)).reshape(NX, NY)  8.39 us
    concatenate x3, other arithmetic, with_halo(): jnp.concatenate([lax.ppermute(tail, axis, [(i, (i + 1) % count) for i in...  5.74 us
    sub x3, other arithmetic, laplace_rim(): return summed - 6.0 * center  5.14 us
    slice x2, local copies, waits for them, and re-layouts, with_halo(): lax.slice_in_dim(cells, cells.shape[dim] - width, cells.shape[dim], axis=...  4.61 us
    reduce_sum x1, other arithmetic, patch_total(): return jnp.sum(field.reshape(PX, SX, PY, SY), axis=(1, 3))  4.01 us
  transfers between devices with their start and end apart: 6, of which 0 were waited for; matrix products, arithmetic and copies ran while one was open for 31% of the time, Pallas kernels for 0%

commit v1 on v0

v1 whole, which is shorter than its diff:
```python
import functools

import jax
import jax.numpy as jnp
from jax import lax
from jax.experimental import pallas as pl
from jax.experimental.pallas import tpu as pltpu
from jax.sharding import PartitionSpec as P

feed_rate = 0.035
substrate_diffusion = 0.16
activator_diffusion = 0.08

ROWS = 32
VMEM = pl.BlockSpec(memory_space=pltpu.VMEM)
EXACT = lax.Precision.HIGHEST


def stencil(load, step, rows, total):
    first = pl.multiple_of(step * rows, rows)
    here = load(first, rows)
    above = load(pl.multiple_of(jnp.maximum(first - 8, 0), 8), 8)
    below = load(pl.multiple_of(jnp.minimum(first + rows, total - 8), 8), 8)
    above = jnp.where(step > 0, above, 0.0)
    below = jnp.where(first + rows < total, below, 0.0)
    tall = jnp.concatenate([above, here, below], axis=0)
    up = pltpu.roll(tall, 1, 0)[8 : 8 + rows]
    down = pltpu.roll(tall, rows + 15, 0)[8 : 8 + rows]
    columns = here.shape[1]
    lane = lax.broadcasted_iota(jnp.int32, here.shape, 1)
    left = jnp.where(lane == 0, 0.0, pltpu.roll(here, 1, 1))
    right = jnp.where(lane == columns - 1, 0.0, pltpu.roll(here, columns - 1, 1))
    return here, (up + down) + (left + right)


def plane(ref, *lead):
    return lambda start, size: ref[(*lead, pl.ds(start, size), slice(None))]


def spread_matrix(cells, patches):
    row = lax.broadcasted_iota(jnp.int32, (cells, patches), 0)
    column = lax.broadcasted_iota(jnp.int32, (cells, patches), 1)
    return jnp.where(row // (cells // patches) == column, 1.0, 0.0)


def gather_matrix(patches, cells):
    row = lax.broadcasted_iota(jnp.int32, (patches, cells), 0)
    column = lax.broadcasted_iota(jnp.int32, (patches, cells), 1)
    return jnp.where(column // (cells // patches) == row, 1.0, 0.0)


def exact_dot(a, b):
    return jnp.dot(a, b, precision=EXACT, preferred_element_type=jnp.float32)


def local_kernel(sides, ck, ad, rate, pert, part, decay, grad_cells, far_mid):
    near = 1 - lax.rem(lax.axis_index("slab"), 2)
    slots = (near, 1 - near)
    total, columns = ck.shape[3:]
    table = rate[...] * (1.0 + pert[0])
    decay[...] = exact_dot(
        exact_dot(spread_matrix(total, table.shape[0]), table),
        gather_matrix(table.shape[1], columns),
    )

    def rows(step, carry):
        here = pl.ds(pl.multiple_of(step * ROWS, ROWS), ROWS)
        loss = decay[here, :] + feed_rate
        fields = {}
        for name, ref, index in (("u", ck, 0), ("v", ck, 1), ("a", ad, 0), ("b", ad, 1)):
            for s in range(2):
                fields[name, s] = stencil(plane(ref, 0, index, slots[s]), step, ROWS, total)
        lap = {
            (n, s): ring + fields[n, 1 - s][0] - 6.0 * mid for (n, s), (mid, ring) in fields.items()
        }
        cells = 0.0
        for s in range(2):
            u, v, a, b = (fields[n, s][0] for n in "uvab")
            reaction = u * v * v
            u_new = u + substrate_diffusion * lap["u", s] - reaction + feed_rate * (1.0 - u)
            v_new = v + activator_diffusion * lap["v", s] + reaction - loss * v
            alpha = a + substrate_diffusion * lap["a", s] - feed_rate * a
            beta = b + activator_diffusion * lap["b", s] - loss * b
            gap = b - a
            if s < sides:
                part[s, 0, here, :] = u_new
                part[s, 1, here, :] = v_new
                part[s, 2, here, :] = alpha
                part[s, 3, here, :] = beta
                part[s, 4, here, :] = gap
            else:
                alpha = alpha + v_new * v_new * gap
                beta = beta + 2.0 * (u_new * v_new) * gap
                far_mid[0, here, :] = alpha
                far_mid[1, here, :] = beta
            cells = cells + (v_new * b + v * beta)
        grad_cells[here, :] = cells
        return carry

    lax.fori_loop(0, total // ROWS, rows, 0)


def react_kernel(sides, share, *refs):
    part, grad_cells, rate, pert = refs[:4]
    halo, state, late = refs[4 : 4 + sides], refs[4 + sides : 4 + 2 * sides], refs[4 + 2 * sides : 4 + 3 * sides]
    alpha, beta, grad, cells = refs[4 + 3 * sides :]
    total, columns = grad_cells.shape

    def rows(step, carry):
        here = pl.ds(pl.multiple_of(step * ROWS, ROWS), ROWS)
        sum_cells = grad_cells[here, :]
        for s in range(sides):
            halo_v = halo[s][1, here, :]
            u_mid = part[s, 0, here, :] + substrate_diffusion * halo[s][0, here, :]
            v_mid = part[s, 1, here, :] + activator_diffusion * halo_v
            gap = part[s, 4, here, :]
            extra = 2.0 * (u_mid * v_mid) * gap
            alpha[s, here, :] = part[s, 2, here, :] + v_mid * v_mid * gap
            beta[s, here, :] = part[s, 3, here, :] + extra
            sum_cells = sum_cells + (
                (2.0 * activator_diffusion) * halo_v * late[s][here, :] + state[s][1, here, :] * extra
            )
        cells[here, :] = sum_cells
        return carry

    lax.fori_loop(0, total // ROWS, rows, 0)
    patches = rate.shape
    summed = exact_dot(
        exact_dot(gather_matrix(patches[0], total), cells[...]),
        spread_matrix(columns, patches[1]),
    )
    grad[...] = summed * (1.0 + pert[0]) * (-share)


def last_kernel(sides, ck, decay, near_a, near_b, far_a, far_b, early, *refs):
    near = 1 - lax.rem(lax.axis_index("slab"), 2)
    total = decay.shape[0]
    mids = ((near_a, near_b), (far_a, far_b))
    outs = refs[:2]

    def rows(step, carry):
        here = pl.ds(pl.multiple_of(step * ROWS, ROWS), ROWS)
        loss = decay[here, :] + feed_rate
        found = [[stencil(plane(ref), step, ROWS, total) for ref in pair] for pair in mids]
        for s in range(2):
            slot = near if s == 0 else 1 - near
            (a, ring_a), (b, ring_b) = found[s]
            lap_a = ring_a + found[1 - s][0][0] - 6.0 * a
            lap_b = ring_b + found[1 - s][1][0] - 6.0 * b
            u = ck[0, 0, slot, here, :]
            v = ck[0, 1, slot, here, :]
            gap = b - a
            outs[s][0, here, :] = a + substrate_diffusion * lap_a - feed_rate * a + v * v * gap
            outs[s][1, here, :] = b + activator_diffusion * lap_b - loss * b + 2.0 * (u * v) * gap
        return carry

    lax.fori_loop(0, total // ROWS, rows, 0)
    if sides == 1:
        copy = pltpu.make_async_copy(refs[1], early.at[0, :, 1 - near], refs[2])
        copy.start()
        copy.wait()


def call(body, name, outs, flops, args, scratch=(), spaces=None):
    return pl.pallas_call(
        body,
        name=name,
        out_shape=[jax.ShapeDtypeStruct(shape, jnp.float32) for shape in outs],
        in_specs=[VMEM] * len(args),
        out_specs=spaces or [VMEM] * len(outs),
        scratch_shapes=list(scratch),
        compiler_params=pltpu.CompilerParams(vmem_limit_bytes=16 << 20),
        cost_estimate=pl.CostEstimate(flops=flops, bytes_accessed=1 << 20, transcendentals=0),
    )(*args)


def exchange(near, far, sides):
    count = lax.axis_size("slab")
    swaps = []
    for side, value in zip(range(sides), (near, far)):
        pairs = [(i, i + 1) for i in range(side, count - 1, 2)]
        swaps.append(lax.ppermute(value, "slab", pairs + [(j, i) for i, j in pairs]))
    return swaps


def butterfly(value, axis):
    count = lax.axis_size(axis)
    if count & (count - 1):
        return lax.psum(value, axis)
    bit = 1
    while bit < count:
        value = value + lax.ppermute(value, axis, [(i, i ^ bit) for i in range(count)])
        bit *= 2
    return value


def local(checkpoint, adjoint_late, rate_params, perturbation):
    sides = 1 if lax.axis_size("slab") <= 2 else 2
    near = 1 - lax.rem(lax.axis_index("slab"), 2)
    grid = checkpoint.shape[3:]

    def pick(array, first, size, slot):
        found = lax.dynamic_slice(array, (0, first, slot, 0, 0), (1, size, 1, *grid))
        return found.reshape((size, *grid) if size > 1 else grid)

    slots = [near, 1 - near][:sides]
    uv = [pick(checkpoint, 0, 2, s) for s in slots]
    late_b = [pick(adjoint_late, 1, 1, s) for s in slots]
    late_a = [pick(adjoint_late, 0, 1, s) for s in slots]
    halo_uv = exchange(uv[0], uv[-1], sides)
    halo_b = exchange(late_b[0], late_b[-1], sides)
    halo_a = exchange(late_a[0], late_a[-1], sides)

    part, decay, grad_cells, far_mid = call(
        functools.partial(local_kernel, sides),
        "local_terms",
        [(sides, 5, *grid), grid, grid, (2, *grid)],
        1 << 28,
        (checkpoint, adjoint_late, rate_params, perturbation),
    )

    share = 1.0 / lax.axis_size("member")
    alpha, beta, grad = call(
        functools.partial(react_kernel, sides, share),
        "reaction",
        [(sides, *grid), (sides, *grid), rate_params.shape],
        1 << 26,
        (part, grad_cells, rate_params, perturbation, *halo_uv, *uv, *late_b),
        [pltpu.VMEM(grid, jnp.float32)],
    )

    mid_b = [beta[s] + activator_diffusion * halo_b[s] for s in range(sides)]
    halo_mid_b = exchange(mid_b[0], mid_b[-1], sides)
    mid_a = [alpha[s] + substrate_diffusion * halo_a[s] for s in range(sides)]
    halo_mid_a = exchange(mid_a[0], mid_a[-1], sides)
    if sides == 1:
        mid_a.append(far_mid[0])
        mid_b.append(far_mid[1])

    whole = [(2, *grid)] * sides
    early, *partial = call(
        functools.partial(last_kernel, sides),
        "last_step",
        [checkpoint.shape, *whole],
        1 << 27,
        (checkpoint, decay, mid_a[0], mid_b[0], mid_a[1], mid_b[1]),
        [pltpu.VMEM((2, *grid), jnp.float32), pltpu.SemaphoreType.DMA] if sides == 1 else [],
        [pl.BlockSpec(memory_space=pl.ANY)] + [VMEM] * sides,
    )
    grad = butterfly(butterfly(grad, "member"), "slab")

    for field, rate, halo in (
        (1, activator_diffusion, halo_mid_b),
        (0, substrate_diffusion, halo_mid_a),
    ):
        for s in range(sides):
            plane_out = partial[s][field] + rate * halo[s]
            early = lax.dynamic_update_slice(early, plane_out[None, None, None], (0, field, slots[s], 0, 0))
    return early, grad


def solution(mesh):
    return jax.shard_map(
        local,
        mesh=mesh,
        in_specs=(
            P("member", None, "slab", None, None),
            P("member", None, "slab", None, None),
            P(),
            P("member", None, None),
        ),
        out_specs=(P("member", None, "slab", None, None), P()),
        check_vma=False,
    )
```

time: 110 us -> 42.4 us (0.39)
  blocking collectives: 41 us -> 0 us
  local copies, waits for them, and re-layouts: 29.3 us -> 3.85 us
  other arithmetic: 19.8 us -> 2.19 us
  waiting for transfers between devices: 0.02 us -> 15.6 us
  Pallas kernels: 0 us -> 5.45 us
  starting transfers between devices: 18.8 us -> 14.3 us
    psum x1 -> x0, blocking collectives: 41 us -> none  [local(): lax.psum(patch_total(first_term + second) * factor, ('member', 'slab'))]
    ppermute x6 -> x10, waiting for transfers between devices: 0.02 us -> 15.6 us  [the longest x5 8.15 us: butterfly(): lax.ppermute(value, axis, [(i, i ^ bit) for i in range(count)])]
    add x1 -> x0, local copies, waits for them, and re-layouts: 10.8 us -> none  [local(): first_term + second]
    reshape x1 -> x2, local copies, waits for them, and re-layouts: 8.39 us -> 2.29 us  [pick(): return found.reshape((size, *grid) if size > 1 else grid)]
    concatenate x3 -> x0, other arithmetic: 5.74 us -> none  [with_halo(): jnp.concatenate([lax.ppermute(tail, axis, [(i, (i + 1) % count) for i in...]
    pallas_call x0 -> x3, Pallas kernels: none -> 5.45 us  [call(): pl.pallas_call(body, name=name, out_shape=[jax.ShapeDtypeStruct(shape, jn...]
    sub x3 -> x0, other arithmetic: 5.14 us -> none  [laplace_rim(): return summed - 6.0 * center]
    slice x2 -> x0, local copies, waits for them, and re-layouts: 4.61 us -> none  [with_halo(): lax.slice_in_dim(cells, cells.shape[dim] - width, cells.shape[dim], axis=...]
  transfers between devices with their start and end apart: 6 -> 10, of which waited for: 0 -> 5; matrix products, arithmetic and copies ran while one was open for 31% -> 6% of each run, Pallas kernels for 0% -> 13%
where the time goes in v1:
time: 42.4 us; the launch traced here: 42.1 us
  waiting for transfers between devices  15.6 us (37%)
  starting transfers between devices  14.3 us (34%)
  Pallas kernels  5.45 us (13%)
  local copies, waits for them, and re-layouts  3.85 us (9%)
  other arithmetic  2.19 us (5%)
  between operations  0.73 us (2%)
    ppermute x5, waiting for transfers between devices, butterfly(): lax.ppermute(value, axis, [(i, i ^ bit) for i in range(count)])  8.15 us
    ppermute x5, starting transfers between devices, exchange(): lax.ppermute(value, 'slab', pairs + [(j, i) for i, j in pairs])  7.45 us
    ppermute x5, waiting for transfers between devices, exchange(): lax.ppermute(value, 'slab', pairs + [(j, i) for i, j in pairs])  7.43 us
    ppermute x5, starting transfers between devices, butterfly(): lax.ppermute(value, axis, [(i, i ^ bit) for i in range(count)])  6.88 us
    pallas_call x3, Pallas kernels, call(): pl.pallas_call(body, name=name, out_shape=[jax.ShapeDtypeStruct(shape, jn...  5.45 us
    reshape x2, local copies, waits for them, and re-layouts, pick(): return found.reshape((size, *grid) if size > 1 else grid)  2.29 us
    unnamed x8, local copies, waits for them, and re-layouts  1.52 us
    dynamic_update_slice x2, other arithmetic, local(): lax.dynamic_update_slice(early, plane_out[None, None, None], (0, field, s...  1.47 us
  transfers between devices with their start and end apart: 10, of which 5 were waited for; matrix products, arithmetic and copies ran while one was open for 6% of the time, Pallas kernels for 13%

profile of v1, /device:TPU:0, one launch (start us, length us, event | category | flops | bytes accessed | tf_op | source)
XLA Modules:
  0.0 42.1 jit_solution(6484219483658493780)
XLA Ops:
  0.6 0.0 copy-start
  0.6 0.0 copy-start.1
  0.7 1.2 %dynamic-slice_bitcast_fusion.refs_5_ = f32[2,256,256]{2,1,0:T(8,128)S(1)} fusion(f32[1,2,2,256,256]{4,3,2,1,0:T(8,128)} %ck.3, s32[]{:T(128)S(6)} %select_n.2), kind=kLoop, calls=%fused_computation | loop fusion | bytes 1048580 | tf_op jit(solution)/shard_map/reshape | solution.py:204
  1.9 3.0 %collective-permute-start = (f32[2,256,256]{2,1,0:T(8,128)S(1)}, f32[2,256,256]{2,1,0:T(8,128)S(1)}, u32[]{:S(2)}, u32[]{:S(2)}) collective-permute-start(f32[2,256,256]{2,1,0:T(8,128)S(1)} %dynamic-slice_bitcast_fusion.refs_5_), channel_id=1, source_target_pairs={{0,1},{1,0},{2,3},{3,2},{4,5},{5,4},{6,7},{7,6},{8,9},{9,8},{10,11... | collective-permute-start | bytes 1572872 | tf_op jit(solution)/shard_map/ppermute | solution.py:182
  4.9 1.1 %dynamic-slice_bitcast_fusion.1 = (f32[256,256]{1,0:T(8,128)S(1)}, f32[256,256]{1,0:T(8,128)S(1)}) fusion(f32[1,2,2,256,256]{4,3,2,1,0:T(8,128)} %ad.1, s32[]{:T(128)S(6)} %select_n.2), kind=kLoop, calls=%fused_computation.9 | loop fusion | bytes 1048580 | tf_op jit(solution)/shard_map/reshape | solution.py:204
  6.0 0.1 collective-permute-start.2
  6.1 0.0 copy-done
  6.1 0.0 copy-done.1
  6.1 0.0 copy-start.2
  6.1 0.7 %copy-done.2 = f32[64,64]{1,0:T(8,128)S(1)} copy-done((f32[64,64]{1,0:T(8,128)S(1)}, f32[64,64]{1,0:T(8,128)}, u32[]{:S(2)}) %copy-start.2) | copy-done | bytes 16408
  6.8 0.0 copy-start.3
  6.8 0.8 %copy-done.3 = f32[1,64,64]{2,1,0:T(8,128)S(1)} copy-done((f32[1,64,64]{2,1,0:T(8,128)S(1)}, f32[1,64,64]{2,1,0:T(8,128)}, u32[]{:S(2)}) %copy-start.3) | copy-done | bytes 16408
  7.6 2.7 %local_terms.1 = (f32[1,5,256,256]{3,2,1,0:T(8,128)S(1)}, f32[256,256]{1,0:T(8,128)S(1)}, f32[256,256]{1,0:T(8,128)S(1)}, f32[2,256,256]{2,1,0:T(8,128)S(1)}) custom-call(f32[1,2,2,256,256]{4,3,2,1,0:T(8,128)S(1)} %copy-done, f32[1,2,2,256,256]{4,3,2,1,0:T(8,128)S(1)} %copy-done.1, f32[64,64]{1,0:T(8,128)S(1)} %copy-done.2, f32[1,64,64]{2,1,0:T(8,128)S(1)} %copy-done.3), custom_call_target="tpu_custom_call" | custom-call | flops 268435456 | bytes 1048576 | tf_op jit(solution)/shard_map/local_terms/pallas_call | solution.py:165
  10.3 7.4 %collective-permute-done.refs_4_ = f32[2,256,256]{2,1,0:T(8,128)S(1)} collective-permute-done((f32[2,256,256]{2,1,0:T(8,128)S(1)}, f32[2,256,256]{2,1,0:T(8,128)S(1)}, u32[]{:S(2)}, u32[]{:S(2)}) %collective-permute-start) | collective-permute-done | bytes 524320 | tf_op jit(solution)/shard_map/ppermute | solution.py:182
  17.7 0.7 %reaction.1 = (f32[1,256,256]{2,1,0:T(8,128)S(1)}, f32[1,256,256]{2,1,0:T(8,128)S(1)}, f32[64,64]{1,0:T(8,128)S(1)}) custom-call(f32[1,5,256,256]{3,2,1,0:T(8,128)S(1)} %get-tuple-element.12.refs_0_, f32[256,256]{1,0:T(8,128)S(1)} %get-tuple-element.13.refs_1_, f32[64,64]{1,0:T(8,128)S(1)} %copy-done.2, f32[1,64,64]{2,1,0:T(8,128)S(1)} %copy-done.3, ...), custom_call_target="tpu_custom_call" | custom-call | flops 67108864 | bytes 1048576 | tf_op jit(solution)/shard_map/reaction/pallas_call | solution.py:165
  18.4 0.1 collective-permute-start.5
  18.5 2.1 %collective-permute-start.1 = (f32[256,256]{1,0:T(8,128)S(1)}, f32[256,256]{1,0:T(8,128)S(1)}, u32[]{:S(2)}, u32[]{:S(2)}) collective-permute-start(f32[256,256]{1,0:T(8,128)S(1)} %get-tuple-element.20), channel_id=1, source_target_pairs={{0,1},{1,0},{2,3},{3,2},{4,5},{5,4},{6,7},{7,6},{8,9},{9,8},{10,11... | collective-permute-start | bytes 786440 | tf_op jit(solution)/shard_map/ppermute | solution.py:182
  20.6 0.0 collective-permute-done.5
  20.6 1.6 %collective-permute-start.6 = (f32[64,64]{1,0:T(8,128)S(1)}, f32[64,64]{1,0:T(8,128)S(1)}, u32[]{:S(2)}, u32[]{:S(2)}) collective-permute-start(f32[64,64]{1,0:T(8,128)S(1)} %add.40), channel_id=1, source_target_pairs={{0,4},{2,6},{4,0},{6,2},{8,12},{10,14},{12,8},{14,10},{16,20},{18,... | collective-permute-start | bytes 49160 | tf_op jit(solution)/shard_map/ppermute | solution.py:192
  22.2 2.4 %collective-permute-done.6 = f32[64,64]{1,0:T(8,128)S(1)} collective-permute-done((f32[64,64]{1,0:T(8,128)S(1)}, f32[64,64]{1,0:T(8,128)S(1)}, u32[]{:S(2)}, u32[]{:S(2)}) %collective-permute-start.6) | collective-permute-done | bytes 16416 | tf_op jit(solution)/shard_map/ppermute | solution.py:192
  24.6 1.6 %collective-permute-start.7 = (f32[64,64]{1,0:T(8,128)S(1)}, f32[64,64]{1,0:T(8,128)S(1)}, u32[]{:S(2)}, u32[]{:S(2)}) collective-permute-start(f32[64,64]{1,0:T(8,128)S(1)} %add.41), channel_id=1, source_target_pairs={{0,8},{2,10},{4,12},{6,14},{8,0},{10,2},{12,4},{14,6},{16,24},{18,... | collective-permute-start | bytes 49160 | tf_op jit(solution)/shard_map/ppermute | solution.py:192
  26.2 0.0 collective-permute-done.2
  26.2 1.1 %collective-permute-start.3 = (f32[256,256]{1,0:T(8,128)S(1)}, f32[256,256]{1,0:T(8,128)S(1)}, u32[]{:S(2)}, u32[]{:S(2)}) collective-permute-start(f32[256,256]{1,0:T(8,128)S(1)} %bitcast_add_fusion.2.near_b), channel_id=1, source_target_pairs={{0,1},{1,0},{2,3},{3,2},{4,5},{5,4},{6,7},{7,6},{8,9},{9,8},{10,11... | collective-permute-start | bytes 786440 | tf_op jit(solution)/shard_map/ppermute | solution.py:182
  27.3 1.2 %collective-permute-done.7 = f32[64,64]{1,0:T(8,128)S(1)} collective-permute-done((f32[64,64]{1,0:T(8,128)S(1)}, f32[64,64]{1,0:T(8,128)S(1)}, u32[]{:S(2)}, u32[]{:S(2)}) %collective-permute-start.7) | collective-permute-done | bytes 16416 | tf_op jit(solution)/shard_map/ppermute | solution.py:192
  28.5 2.6 %collective-permute-start.8 = (f32[64,64]{1,0:T(8,128)S(1)}, f32[64,64]{1,0:T(8,128)S(1)}, u32[]{:S(2)}, u32[]{:S(2)}) collective-permute-start(f32[64,64]{1,0:T(8,128)S(1)} %add.42), channel_id=1, source_target_pairs={{0,16},{2,18},{4,20},{6,22},{8,24},{10,26},{12,28},{14,30},{16,0},... | collective-permute-start | bytes 49160 | tf_op jit(solution)/shard_map/ppermute | solution.py:192
  31.1 0.0 collective-permute-done.1
  31.1 1.1 %collective-permute-start.4 = (f32[256,256]{1,0:T(8,128)S(1)}, f32[256,256]{1,0:T(8,128)S(1)}, u32[]{:S(2)}, u32[]{:S(2)}) collective-permute-start(f32[256,256]{1,0:T(8,128)S(1)} %bitcast_add_fusion.3.near_a), channel_id=1, source_target_pairs={{0,1},{1,0},{2,3},{3,2},{4,5},{5,4},{6,7},{7,6},{8,9},{9,8},{10,11... | collective-permute-start | bytes 786440 | tf_op jit(solution)/shard_map/ppermute | solution.py:182
  32.3 1.1 %collective-permute-done.8 = f32[64,64]{1,0:T(8,128)S(1)} collective-permute-done((f32[64,64]{1,0:T(8,128)S(1)}, f32[64,64]{1,0:T(8,128)S(1)}, u32[]{:S(2)}, u32[]{:S(2)}) %collective-permute-start.8) | collective-permute-done | bytes 16416 | tf_op jit(solution)/shard_map/ppermute | solution.py:192
  33.3 1.1 %collective-permute-start.9 = (f32[64,64]{1,0:T(8,128)S(1)}, f32[64,64]{1,0:T(8,128)S(1)}, u32[]{:S(2)}, u32[]{:S(2)}) collective-permute-start(f32[64,64]{1,0:T(8,128)S(1)} %add.43), channel_id=1, source_target_pairs={{0,1},{1,0},{2,3},{3,2},{4,5},{5,4},{6,7},{7,6},{8,9},{9,8},{10,11... | collective-permute-start | bytes 49160 | tf_op jit(solution)/shard_map/ppermute | solution.py:192
  34.4 2.1 %last_step.1 = (f32[1,2,2,256,256]{4,3,2,1,0:T(8,128)}, f32[2,256,256]{2,1,0:T(8,128)S(1)}) custom-call(f32[1,2,2,256,256]{4,3,2,1,0:T(8,128)S(1)} %copy-done, f32[256,256]{1,0:T(8,128)S(1)} %get-tuple-element.11.decay, f32[256,256]{1,0:T(8,128)S(1)} %bitcast_add_fusion.3.near_a, f32[256,256]{1,0:T(8,128)S(1)} %bitcast_add_fusion.2.near_b, ...), custom_call_target="tpu_custom_call" | custom-call | flops 134217728 | bytes 1048576 | tf_op jit(solution)/shard_map/last_step/pallas_call | solution.py:165
  36.5 3.5 %collective-permute-done.9 = f32[64,64]{1,0:T(8,128)S(1)} collective-permute-done((f32[64,64]{1,0:T(8,128)S(1)}, f32[64,64]{1,0:T(8,128)S(1)}, u32[]{:S(2)}, u32[]{:S(2)}) %collective-permute-start.9) | collective-permute-done | bytes 16416 | tf_op jit(solution)/shard_map/ppermute | solution.py:192
  40.0 0.6 %add.44 = f32[64,64]{1,0:T(8,128)} add(f32[64,64]{1,0:T(8,128)S(1)} %add.43, f32[64,64]{1,0:T(8,128)S(1)} %collective-permute-done.9) | non-fusion elementwise | flops 4096 | bytes 49152 | tf_op jit(solution)/shard_map/add | solution.py:192
  40.6 0.0 collective-permute-done.3
  40.6 0.7 %bitcast_dynamic-update-slice_fusion.1 = f32[1,2,2,256,256]{4,3,2,1,0:T(8,128)} fusion(f32[1,2,2,256,256]{4,3,2,1,0:T(8,128)} %get-tuple-element.17, s32[]{:T(128)S(6)} %select_n.2, f32[256,256]{1,0:T(8,128)S(1)} %collective-permute-done.3, f32[2,256,256]{2,1,0:T(8,128)S(1)} %get-tuple-element.18), kind=kLoop, calls=%fused_computation.3 | loop fusion | flops 131072 | bytes 786436 | tf_op jit(solution)/shard_map/dynamic_update_slice | solution.py:258
  41.4 0.0 collective-permute-done.4
  41.4 0.7 %bitcast_dynamic-update-slice_fusion = f32[1,2,2,256,256]{4,3,2,1,0:T(8,128)} fusion(f32[1,2,2,256,256]{4,3,2,1,0:T(8,128)} %bitcast_dynamic-update-slice_fusion.1, s32[]{:T(128)S(6)} %select_n.2, f32[256,256]{1,0:T(8,128)S(1)} %collective-permute-done.4, f32[2,256,256]{2,1,0:T(8,128)S(1)} %get-tuple-element.18), kind=kLoop, calls=%fused_computation.1 | loop fusion | flops 131072 | bytes 786436 | tf_op jit(solution)/shard_map/dynamic_update_slice | solution.py:258
  (7 shorter events, 0.1 us)
Async XLA Ops:
  0.6 5.4 %copy-start = (f32[1,2,2,256,256]{4,3,2,1,0:T(8,128)S(1)}, f32[1,2,2,256,256]{4,3,2,1,0:T(8,128)}, u32[]{:S(2)}) copy-start(f32[1,2,2,256,256]{4,3,2,1,0:T(8,128)} %ck.3) | copy-start | bytes 3145732
  0.6 5.4 %copy-start.1 = (f32[1,2,2,256,256]{4,3,2,1,0:T(8,128)S(1)}, f32[1,2,2,256,256]{4,3,2,1,0:T(8,128)}, u32[]{:S(2)}) copy-start(f32[1,2,2,256,256]{4,3,2,1,0:T(8,128)} %ad.1) | copy-start | bytes 3145732
  1.9 15.8 %collective-permute-start = (f32[2,256,256]{2,1,0:T(8,128)S(1)}, f32[2,256,256]{2,1,0:T(8,128)S(1)}, u32[]{:S(2)}, u32[]{:S(2)}) collective-permute-start(f32[2,256,256]{2,1,0:T(8,128)S(1)} %dynamic-slice_bitcast_fusion.refs_5_), channel_id=1, source_target_pairs={{0,1},{1,0},{2,3},{3,2},{4,5},{5,4},{6,7},{7,6},{8,9},{9,8},{10,11... | collective-permute-start | bytes 1572872 | tf_op jit(solution)/shard_map/ppermute | solution.py:182
  6.0 20.2 %collective-permute-start.2 = (f32[256,256]{1,0:T(8,128)S(1)}, f32[256,256]{1,0:T(8,128)S(1)}, u32[]{:S(2)}, u32[]{:S(2)}) collective-permute-start(f32[256,256]{1,0:T(8,128)S(1)} %get-tuple-element.21.refs_6_), channel_id=1, source_target_pairs={{0,1},{1,0},{2,3},{3,2},{4,5},{5,4},{6,7},{7,6},{8,9},{9,8},{10,11... | collective-permute-start | bytes 786440 | tf_op jit(solution)/shard_map/ppermute | solution.py:182
  6.1 0.8 %copy-start.2 = (f32[64,64]{1,0:T(8,128)S(1)}, f32[64,64]{1,0:T(8,128)}, u32[]{:S(2)}) copy-start(f32[64,64]{1,0:T(8,128)} %refs_2_.1) | copy-start | bytes 49156
  6.8 0.8 %copy-start.3 = (f32[1,64,64]{2,1,0:T(8,128)S(1)}, f32[1,64,64]{2,1,0:T(8,128)}, u32[]{:S(2)}) copy-start(f32[1,64,64]{2,1,0:T(8,128)} %refs_3_.1) | copy-start | bytes 49156
  18.4 2.2 %collective-permute-start.5 = (f32[64,64]{1,0:T(8,128)S(1)}, f32[64,64]{1,0:T(8,128)S(1)}, u32[]{:S(2)}, u32[]{:S(2)}) collective-permute-start(f32[64,64]{1,0:T(8,128)S(1)} %get-tuple-element.19), channel_id=1, source_target_pairs={{0,2},{2,0},{4,6},{6,4},{8,10},{10,8},{12,14},{14,12},{16,18},{18,... | collective-permute-start | bytes 49160 | tf_op jit(solution)/shard_map/ppermute | solution.py:192
  18.5 12.6 %collective-permute-start.1 = (f32[256,256]{1,0:T(8,128)S(1)}, f32[256,256]{1,0:T(8,128)S(1)}, u32[]{:S(2)}, u32[]{:S(2)}) collective-permute-start(f32[256,256]{1,0:T(8,128)S(1)} %get-tuple-element.20), channel_id=1, source_target_pairs={{0,1},{1,0},{2,3},{3,2},{4,5},{5,4},{6,7},{7,6},{8,9},{9,8},{10,11... | collective-permute-start | bytes 786440 | tf_op jit(solution)/shard_map/ppermute | solution.py:182
  20.6 4.0 %collective-permute-start.6 = (f32[64,64]{1,0:T(8,128)S(1)}, f32[64,64]{1,0:T(8,128)S(1)}, u32[]{:S(2)}, u32[]{:S(2)}) collective-permute-start(f32[64,64]{1,0:T(8,128)S(1)} %add.40), channel_id=1, source_target_pairs={{0,4},{2,6},{4,0},{6,2},{8,12},{10,14},{12,8},{14,10},{16,20},{18,... | collective-permute-start | bytes 49160 | tf_op jit(solution)/shard_map/ppermute | solution.py:192
  24.6 3.9 %collective-permute-start.7 = (f32[64,64]{1,0:T(8,128)S(1)}, f32[64,64]{1,0:T(8,128)S(1)}, u32[]{:S(2)}, u32[]{:S(2)}) collective-permute-start(f32[64,64]{1,0:T(8,128)S(1)} %add.41), channel_id=1, source_target_pairs={{0,8},{2,10},{4,12},{6,14},{8,0},{10,2},{12,4},{14,6},{16,24},{18,... | collective-permute-start | bytes 49160 | tf_op jit(solution)/shard_map/ppermute | solution.py:192
  26.2 14.4 %collective-permute-start.3 = (f32[256,256]{1,0:T(8,128)S(1)}, f32[256,256]{1,0:T(8,128)S(1)}, u32[]{:S(2)}, u32[]{:S(2)}) collective-permute-start(f32[256,256]{1,0:T(8,128)S(1)} %bitcast_add_fusion.2.near_b), channel_id=1, source_target_pairs={{0,1},{1,0},{2,3},{3,2},{4,5},{5,4},{6,7},{7,6},{8,9},{9,8},{10,11... | collective-permute-start | bytes 786440 | tf_op jit(solution)/shard_map/ppermute | solution.py:182
  28.5 4.8 %collective-permute-start.8 = (f32[64,64]{1,0:T(8,128)S(1)}, f32[64,64]{1,0:T(8,128)S(1)}, u32[]{:S(2)}, u32[]{:S(2)}) collective-permute-start(f32[64,64]{1,0:T(8,128)S(1)} %add.42), channel_id=1, source_target_pairs={{0,16},{2,18},{4,20},{6,22},{8,24},{10,26},{12,28},{14,30},{16,0},... | collective-permute-start | bytes 49160 | tf_op jit(solution)/shard_map/ppermute | solution.py:192
  31.1 10.2 %collective-permute-start.4 = (f32[256,256]{1,0:T(8,128)S(1)}, f32[256,256]{1,0:T(8,128)S(1)}, u32[]{:S(2)}, u32[]{:S(2)}) collective-permute-start(f32[256,256]{1,0:T(8,128)S(1)} %bitcast_add_fusion.3.near_a), channel_id=1, source_target_pairs={{0,1},{1,0},{2,3},{3,2},{4,5},{5,4},{6,7},{7,6},{8,9},{9,8},{10,11... | collective-permute-start | bytes 786440 | tf_op jit(solution)/shard_map/ppermute | solution.py:182
  33.3 6.7 %collective-permute-start.9 = (f32[64,64]{1,0:T(8,128)S(1)}, f32[64,64]{1,0:T(8,128)S(1)}, u32[]{:S(2)}, u32[]{:S(2)}) collective-permute-start(f32[64,64]{1,0:T(8,128)S(1)} %add.43), channel_id=1, source_target_pairs={{0,1},{1,0},{2,3},{3,2},{4,5},{5,4},{6,7},{7,6},{8,9},{9,8},{10,11... | collective-permute-start | bytes 49160 | tf_op jit(solution)/shard_map/ppermute | solution.py:192

commit v2 on v1

v2 whole, which is shorter than its diff:
```python
import functools

import jax
import jax.numpy as jnp
from jax import lax
from jax.experimental import pallas as pl
from jax.experimental.pallas import tpu as pltpu
from jax.sharding import PartitionSpec as P


feed_rate = 0.035
substrate_diffusion = 0.16
activator_diffusion = 0.08


ROWS = 32
PIECES = 2
VMEM = pl.BlockSpec(memory_space=pltpu.VMEM)
HBM = pl.BlockSpec(memory_space=pl.ANY)
STAY = pl.BlockSpec(memory_space=pltpu.HBM)
EXACT = lax.Precision.HIGHEST


def stencil(load, step, rows, total):
    first = pl.multiple_of(step * rows, rows)
    here = load(first, rows)
    above = load(pl.multiple_of(jnp.maximum(first - 8, 0), 8), 8)
    below = load(pl.multiple_of(jnp.minimum(first + rows, total - 8), 8), 8)
    above = jnp.where(step > 0, above, 0.0)
    below = jnp.where(first + rows < total, below, 0.0)
    tall = jnp.concatenate([above, here, below], axis=0)
    up = pltpu.roll(tall, 1, 0)[8 : 8 + rows]
    down = pltpu.roll(tall, rows + 15, 0)[8 : 8 + rows]
    columns = here.shape[1]
    lane = lax.broadcasted_iota(jnp.int32, here.shape, 1)
    left = jnp.where(lane == 0, 0.0, pltpu.roll(here, 1, 1))
    right = jnp.where(lane == columns - 1, 0.0, pltpu.roll(here, columns - 1, 1))
    return here, (up + down) + (left + right)


def plane(ref, *lead):
    return lambda start, size: ref[(*lead, pl.ds(start, size), slice(None))]


def spread_matrix(cells, patches):
    row = lax.broadcasted_iota(jnp.int32, (cells, patches), 0)
    column = lax.broadcasted_iota(jnp.int32, (cells, patches), 1)
    return jnp.where(row // (cells // patches) == column, 1.0, 0.0)


def gather_matrix(patches, cells):
    row = lax.broadcasted_iota(jnp.int32, (patches, cells), 0)
    column = lax.broadcasted_iota(jnp.int32, (patches, cells), 1)
    return jnp.where(column // (cells // patches) == row, 1.0, 0.0)


def exact_dot(a, b):
    return jnp.dot(a, b, precision=EXACT, preferred_element_type=jnp.float32)


def local_kernel(sides, state, late, rate, pert, part, decay, grad_cells, far_mid, products, ck, ad, sems):
    near = 1 - lax.rem(lax.axis_index("slab"), 2)
    copies = [pltpu.make_async_copy(state, ck, sems.at[0]), pltpu.make_async_copy(late, ad, sems.at[1])]
    for copy in copies:
        copy.start()
    slots = (near, 1 - near)
    total, columns = ck.shape[3:]
    table = rate[...] * (1.0 + pert[0])
    decay[...] = exact_dot(
        exact_dot(spread_matrix(total, table.shape[0]), table),
        gather_matrix(table.shape[1], columns),
    )

    for copy in copies:
        copy.wait()

    def rows(step, carry):
        here = pl.ds(pl.multiple_of(step * ROWS, ROWS), ROWS)
        loss = decay[here, :] + feed_rate
        fields = {}
        for name, ref, index in (("u", ck, 0), ("v", ck, 1), ("a", ad, 0), ("b", ad, 1)):
            for s in range(2):
                fields[name, s] = stencil(plane(ref, 0, index, slots[s]), step, ROWS, total)
        lap = {
            (n, s): ring + fields[n, 1 - s][0] - 6.0 * mid for (n, s), (mid, ring) in fields.items()
        }
        cells = 0.0
        for s in range(2):
            u, v, a, b = (fields[n, s][0] for n in "uvab")
            reaction = u * v * v
            u_new = u + substrate_diffusion * lap["u", s] - reaction + feed_rate * (1.0 - u)
            v_new = v + activator_diffusion * lap["v", s] + reaction - loss * v
            alpha = a + substrate_diffusion * lap["a", s] - feed_rate * a
            beta = b + activator_diffusion * lap["b", s] - loss * b
            gap = b - a
            products[s, 0, here, :] = v * v
            products[s, 1, here, :] = 2.0 * (u * v)
            if s < sides:
                part[s, 0, here, :] = u_new
                part[s, 1, here, :] = v_new
                part[s, 2, here, :] = alpha
                part[s, 3, here, :] = beta
                part[s, 4, here, :] = gap
            else:
                alpha = alpha + v_new * v_new * gap
                beta = beta + 2.0 * (u_new * v_new) * gap
                far_mid[0, here, :] = alpha
                far_mid[1, here, :] = beta
            cells = cells + (v_new * b + v * beta)
        grad_cells[here, :] = cells
        return carry

    lax.fori_loop(0, total // ROWS, rows, 0)


def react_kernel(sides, share, *refs):
    part, grad_cells, rate, pert = refs[:4]
    halo_u, halo_v, state_v, late_b = (refs[4 + i * sides : 4 + (i + 1) * sides] for i in range(4))
    alpha, beta, grad, cells = refs[4 + 4 * sides :]
    total, columns = grad_cells.shape

    def rows(step, carry):
        here = pl.ds(pl.multiple_of(step * ROWS, ROWS), ROWS)
        sum_cells = grad_cells[here, :]
        for s in range(sides):
            v_in = halo_v[s][here, :]
            u_mid = part[s, 0, here, :] + substrate_diffusion * halo_u[s][here, :]
            v_mid = part[s, 1, here, :] + activator_diffusion * v_in
            gap = part[s, 4, here, :]
            extra = 2.0 * (u_mid * v_mid) * gap
            alpha[s, here, :] = part[s, 2, here, :] + v_mid * v_mid * gap
            beta[s, here, :] = part[s, 3, here, :] + extra
            sum_cells = sum_cells + (
                (2.0 * activator_diffusion) * v_in * late_b[s][here, :] + state_v[s][here, :] * extra
            )
        cells[here, :] = sum_cells
        return carry

    lax.fori_loop(0, total // ROWS, rows, 0)
    patches = rate.shape
    summed = exact_dot(
        exact_dot(gather_matrix(patches[0], total), cells[...]),
        spread_matrix(columns, patches[1]),
    )
    summed = summed * (1.0 + pert[0]) * (-share)
    tall = grad.shape[0]
    grad[...] = jnp.concatenate(
        [summed[first : first + tall] for first in range(0, patches[0], tall)], axis=1
    )


def last_kernel(sides, products, decay, alpha, beta, *refs):
    near = 1 - lax.rem(lax.axis_index("slab"), 2)
    total = decay.shape[0]

    def middle(base, halo, slot, rate):
        def load(start, size):
            here = pl.ds(start, size)
            return base[slot, here, :] + rate * halo[here, :]

        return load

    mids = [
        (
            middle(alpha, refs[s], s, substrate_diffusion),
            middle(beta, refs[sides + s], s, activator_diffusion),
        )
        for s in range(sides)
    ]
    refs = refs[2 * sides :]
    if sides == 1:
        far_mid, *refs = refs
        mids.append((plane(far_mid, 0), plane(far_mid, 1)))
    early, *outs = refs

    def rows(step, carry):
        here = pl.ds(pl.multiple_of(step * ROWS, ROWS), ROWS)
        loss = decay[here, :] + feed_rate
        found = [[stencil(load, step, ROWS, total) for load in pair] for pair in mids]
        for s in range(2):
            (a, ring_a), (b, ring_b) = found[s]
            lap_a = ring_a + found[1 - s][0][0] - 6.0 * a
            lap_b = ring_b + found[1 - s][1][0] - 6.0 * b
            gap = b - a
            outs[s][0, here, :] = (
                a + substrate_diffusion * lap_a - feed_rate * a + products[s, 0, here, :] * gap
            )
            outs[s][1, here, :] = (
                b + activator_diffusion * lap_b - loss * b + products[s, 1, here, :] * gap
            )
        return carry

    lax.fori_loop(0, total // ROWS, rows, 0)
    if sides == 1:
        copy = pltpu.make_async_copy(outs[1], early.at[0, :, 1 - near], outs[2])
        copy.start()
        copy.wait()


def finish_kernel(sides, before, grad, arrived, *refs):
    near = 1 - lax.rem(lax.axis_index("slab"), 2)
    partial, halo = refs[:sides], refs[sides : 2 * sides]
    early, total, planes, table, sems = refs[2 * sides :]
    copies = []

    def send(source, target):
        copies.append(pltpu.make_async_copy(source, target, sems.at[len(copies)]))
        copies[-1].start()

    rows = planes.shape[1]
    for s in range(sides):
        slot = near if s == 0 else 1 - near
        for first in range(0, rows, rows // PIECES):
            here = pl.ds(first, rows // PIECES)
            planes[s, here, :] = partial[s][0, here, :] + substrate_diffusion * halo[s][here, :]
            send(planes.at[s, here], early.at[0, 0, slot, here])
    tall, columns = grad.shape[0], total.shape[1]
    for fold in range(grad.shape[1] // columns):
        part = slice(fold * columns, (fold + 1) * columns)
        table[fold * tall : (fold + 1) * tall, :] = grad[:, part] + arrived[:, part]
    send(table, total)
    for copy in copies:
        copy.wait()


def call(body, outs, flops, args, scratch=(), writes=None, reads=None, aliases={}):
    return pl.pallas_call(
        body,
        out_shape=[jax.ShapeDtypeStruct(shape, jnp.float32) for shape in outs],
        in_specs=reads or [VMEM] * len(args),
        out_specs=writes or [VMEM] * len(outs),
        input_output_aliases=aliases,
        scratch_shapes=list(scratch),
        compiler_params=pltpu.CompilerParams(vmem_limit_bytes=16 << 20),
        cost_estimate=pl.CostEstimate(flops=flops, bytes_accessed=1 << 20, transcendentals=0),
    )(*args)


def exchange(near, far, sides):
    count = lax.axis_size("slab")
    swaps = []
    for side, value in zip(range(sides), (near, far)):
        pairs = [(i, i + 1) for i in range(side, count - 1, 2)]
        swaps.append(lax.ppermute(value, "slab", pairs + [(j, i) for i, j in pairs]))
    return swaps


def total_of(value):
    last = jnp.zeros_like(value)
    hops = []
    for axis in ("member", "slab"):
        count = lax.axis_size(axis)
        if count & (count - 1):
            value = lax.psum(value, axis)
        else:
            hops += [(axis, count, 1 << bit) for bit in range(count.bit_length() - 1)]
    for index, (axis, count, bit) in enumerate(hops):
        last = lax.ppermute(value, axis, [(i, i ^ bit) for i in range(count)])
        if index + 1 < len(hops):
            value = value + last
    return value, last


def folded(shape):
    fold = max(128 // shape[1], 1)
    return (shape[0] // fold, shape[1] * fold) if shape[0] % (8 * fold) == 0 else shape


def local(checkpoint, adjoint_late, rate_params, perturbation):
    sides = 1 if lax.axis_size("slab") <= 2 else 2
    near = 1 - lax.rem(lax.axis_index("slab"), 2)
    grid = checkpoint.shape[3:]

    def pick(array, field, slot):
        return lax.dynamic_slice(array, (0, field, slot, 0, 0), (1, 1, 1, *grid)).reshape(grid)

    slots = [near, 1 - near][:sides]
    u = [pick(checkpoint, 0, s) for s in slots]
    halo_u = exchange(u[0], u[-1], sides)
    slots, _ = lax.optimization_barrier((slots, u))
    v = [pick(checkpoint, 1, s) for s in slots]
    halo_v = exchange(v[0], v[-1], sides)
    late_b = [pick(adjoint_late, 1, s) for s in slots]
    late_a = [pick(adjoint_late, 0, s) for s in slots]
    halo_b = exchange(late_b[0], late_b[-1], sides)
    halo_a = exchange(late_a[0], late_a[-1], sides)

    part, decay, grad_cells, far_mid, products = call(
        functools.partial(local_kernel, sides),
        [(sides, 5, *grid), grid, grid, (2, *grid), (2, 2, *grid)],
        1 << 28,
        (checkpoint, adjoint_late, rate_params, perturbation),
        [
            pltpu.VMEM(checkpoint.shape, jnp.float32),
            pltpu.VMEM(adjoint_late.shape, jnp.float32),
            pltpu.SemaphoreType.DMA((2,)),
        ],
        reads=[STAY, STAY, VMEM, VMEM],
    )

    share = 1.0 / lax.axis_size("member")
    alpha, beta, grad = call(
        functools.partial(react_kernel, sides, share),
        [(sides, *grid), (sides, *grid), folded(rate_params.shape)],
        1 << 26,
        (part, grad_cells, rate_params, perturbation, *halo_u, *halo_v, *v, *late_b),
        [pltpu.VMEM(grid, jnp.float32)],
    )

    mid_b = [beta[s] + activator_diffusion * halo_b[s] for s in range(sides)]
    halo_mid_b = exchange(mid_b[0], mid_b[-1], sides)
    mid_a = [alpha[s] + substrate_diffusion * halo_a[s] for s in range(sides)]
    halo_mid_a = exchange(mid_a[0], mid_a[-1], sides)

    early, *partial = call(
        functools.partial(last_kernel, sides),
        [checkpoint.shape] + [(2, *grid)] * sides,
        1 << 27,
        (products, decay, alpha, beta, *halo_a, *halo_b, *([far_mid] if sides == 1 else [])),
        [pltpu.VMEM((2, *grid), jnp.float32), pltpu.SemaphoreType.DMA] if sides == 1 else [],
        [HBM] + [VMEM] * sides,
    )
    for s in range(sides):
        done = partial[s][1] + activator_diffusion * halo_mid_b[s]
        early = lax.dynamic_update_slice(early, done[None, None, None], (0, 1, slots[s], 0, 0))
    return call(
        functools.partial(finish_kernel, sides),
        [checkpoint.shape, rate_params.shape],
        1 << 22,
        (early, *total_of(grad), *partial, *halo_mid_a),
        [
            pltpu.VMEM((sides, *grid), jnp.float32),
            pltpu.VMEM(rate_params.shape, jnp.float32),
            pltpu.SemaphoreType.DMA((PIECES * sides + 1,)),
        ],
        [HBM, HBM],
        [HBM] + [VMEM] * (2 + 2 * sides),
        {0: 0},
    )


def solution(mesh):
    return jax.shard_map(
        local,
        mesh=mesh,
        in_specs=(
            P("member", None, "slab", None, None),
            P("member", None, "slab", None, None),
            P(),
            P("member", None, None),
        ),
        out_specs=(P("member", None, "slab", None, None), P()),
        check_vma=False,
    )
```

time: 42.4 us -> 40.6 us (0.958)
  waiting for transfers between devices: 15.6 us -> 12 us
  starting transfers between devices: 14.3 us -> 16.4 us
  other arithmetic: 2.19 us -> 0.83 us
  Pallas kernels: 5.45 us -> 6.45 us
    ppermute x5, waiting for transfers between devices: 8.15 us -> 3.69 us  [total_of(): last = lax.ppermute(value, axis, [(i, i ^ bit) for i in range(count)])]
    ppermute x5 -> x6, starting transfers between devices: 7.45 us -> 9.44 us  [exchange(): lax.ppermute(value, 'slab', pairs + [(j, i) for i, j in pairs])]
    pallas_call x3 -> x4, Pallas kernels: 5.45 us -> 6.45 us  [call(): pl.pallas_call(body, out_shape=[jax.ShapeDtypeStruct(shape, jnp.float32)...]
    ppermute x5 -> x6, waiting for transfers between devices: 7.43 us -> 8.31 us  [exchange(): lax.ppermute(value, 'slab', pairs + [(j, i) for i, j in pairs])]
    reshape x2 -> x3, local copies, waits for them, and re-layouts: 2.29 us -> 3.14 us  [pick(): lax.dynamic_slice(array, (0, field, slot, 0, 0), (1, 1, 1, *grid))]
    unnamed x8, local copies, waits for them, and re-layouts: 1.52 us -> 0.77 us
    dynamic_update_slice x2 -> x1, other arithmetic: 1.47 us -> 0.74 us  [local(): lax.dynamic_update_slice(early, done[None, None, None], (0, 1, slots[s],...]
    add x5 -> x4, other arithmetic: 0.64 us -> 0.02 us  [total_of(): value = value + last]
  transfers between devices with their start and end apart: 10 -> 11, of which waited for: 5 -> 5; matrix products, arithmetic and copies ran while one was open for 6% -> 7% of each run, Pallas kernels for 13% -> 14%
where the time goes in v2:
time: 40.6 us; the launch traced here: 40.3 us
  starting transfers between devices  16.4 us (40%)
  waiting for transfers between devices  12 us (30%)
  Pallas kernels  6.45 us (16%)
  local copies, waits for them, and re-layouts  3.91 us (10%)
  other arithmetic  0.83 us (2%)
  between operations  0.74 us (2%)
    ppermute x6, starting transfers between devices, exchange(): lax.ppermute(value, 'slab', pairs + [(j, i) for i, j in pairs])  9.44 us
    ppermute x6, waiting for transfers between devices, exchange(): lax.ppermute(value, 'slab', pairs + [(j, i) for i, j in pairs])  8.31 us
    ppermute x5, starting transfers between devices, total_of(): last = lax.ppermute(value, axis, [(i, i ^ bit) for i in range(count)])  6.95 us
    pallas_call x4, Pallas kernels, call(): pl.pallas_call(body, out_shape=[jax.ShapeDtypeStruct(shape, jnp.float32)...  6.45 us
    ppermute x5, waiting for transfers between devices, total_of(): last = lax.ppermute(value, axis, [(i, i ^ bit) for i in range(count)])  3.69 us
    reshape x3, local copies, waits for them, and re-layouts, pick(): lax.dynamic_slice(array, (0, field, slot, 0, 0), (1, 1, 1, *grid))  3.14 us
  transfers between devices with their start and end apart: 11, of which 5 were waited for; matrix products, arithmetic and copies ran while one was open for 7% of the time, Pallas kernels for 14%

profile of v2, /device:TPU:0, one launch (start us, length us, event | category | flops | bytes accessed | tf_op | source)
XLA Modules:
  0.0 40.3 jit_solution(8965404935645308023)
XLA Ops:
  0.6 0.0 copy-start
  0.6 0.0 copy-start.1
  0.7 0.0 copy-start.2
  0.7 1.1 %dynamic-slice_bitcast_fusion.3 = f32[256,256]{1,0:T(8,128)S(1)} fusion(f32[1,2,2,256,256]{4,3,2,1,0:T(8,128)} %state.1, s32[]{:T(128)S(6)} %select_n.4), kind=kLoop, calls=%fused_computation.7 | loop fusion | bytes 524292 | tf_op jit(solution)/shard_map/reshape | solution.py:275
  1.8 3.0 %collective-permute-start = (f32[256,256]{1,0:T(8,128)S(1)}, f32[256,256]{1,0:T(8,128)S(1)}, u32[]{:S(2)}, u32[]{:S(2)}) collective-permute-start(f32[256,256]{1,0:T(8,128)S(1)} %dynamic-slice_bitcast_fusion.3), channel_id=1, source_target_pairs={{0,1},{1,0},{2,3},{3,2},{4,5},{5,4},{6,7},{7,6},{8,9},{9,8},{10,11... | collective-permute-start | bytes 786440 | tf_op jit(solution)/shard_map/ppermute | solution.py:244
  4.8 1.0 %dynamic-slice_bitcast_fusion.2.refs_6_ = f32[256,256]{1,0:T(8,128)S(1)} fusion(f32[1,2,2,256,256]{4,3,2,1,0:T(8,128)} %state.1, s32[]{:T(128)S(6)} %select_n.10), kind=kLoop, calls=%fused_computation.6 | loop fusion | bytes 524292 | tf_op jit(solution)/shard_map/reshape | solution.py:275
  5.8 0.1 collective-permute-start.1
  5.9 1.1 %dynamic-slice_bitcast_fusion = (f32[256,256]{1,0:T(8,128)S(1)}, f32[256,256]{1,0:T(8,128)S(1)}) fusion(f32[1,2,2,256,256]{4,3,2,1,0:T(8,128)} %late.1, s32[]{:T(128)S(6)} %select_n.10), kind=kLoop, calls=%fused_computation.4 | loop fusion | bytes 1048580 | tf_op jit(solution)/shard_map/reshape | solution.py:275
  6.9 2.1 %collective-permute-start.3 = (f32[256,256]{1,0:T(8,128)S(1)}, f32[256,256]{1,0:T(8,128)S(1)}, u32[]{:S(2)}, u32[]{:S(2)}) collective-permute-start(f32[256,256]{1,0:T(8,128)S(1)} %get-tuple-element.25.refs_7_), channel_id=1, source_target_pairs={{0,1},{1,0},{2,3},{3,2},{4,5},{5,4},{6,7},{7,6},{8,9},{9,8},{10,11... | collective-permute-start | bytes 786440 | tf_op jit(solution)/shard_map/ppermute | solution.py:244
  9.0 0.1 collective-permute-start.2
  9.1 0.0 copy-done
  9.1 0.0 copy-done.1
  9.1 0.0 copy-done.2
  9.1 0.0 copy-start.3
  9.1 0.8 %copy-done.3 = f32[1,64,64]{2,1,0:T(8,128)S(1)} copy-done((f32[1,64,64]{2,1,0:T(8,128)S(1)}, f32[1,64,64]{2,1,0:T(8,128)}, u32[]{:S(2)}) %copy-start.3) | copy-done | bytes 16408
  9.9 2.8 %shard_map.59 = (f32[1,5,256,256]{3,2,1,0:T(8,128)S(1)}, f32[256,256]{1,0:T(8,128)S(1)}, f32[256,256]{1,0:T(8,128)S(1)}, f32[2,256,256]{2,1,0:T(8,128)S(1)}, f32[2,2,256,256]{3,2,1,0:T(8,128)S(1)}) custom-call(f32[1,2,2,256,256]{4,3,2,1,0:T(8,128)S(1)} %copy-done, f32[1,2,2,256,256]{4,3,2,1,0:T(8,128)S(1)} %copy-done.1, f32[64,64]{1,0:T(8,128)S(1)} %copy-done.2, ...), custom_call_target="tpu_custom_call" | custom-call | flops 268435456 | bytes 1048576 | tf_op jit(solution)/shard_map/pallas_call | solution.py:227
  12.7 4.9 %collective-permute-done.1.refs_5_ = f32[256,256]{1,0:T(8,128)S(1)} collective-permute-done((f32[256,256]{1,0:T(8,128)S(1)}, f32[256,256]{1,0:T(8,128)S(1)}, u32[]{:S(2)}, u32[]{:S(2)}) %collective-permute-start.1) | collective-permute-done | bytes 262176 | tf_op jit(solution)/shard_map/ppermute | solution.py:244
  17.6 0.0 collective-permute-done.refs_4_
  17.6 0.8 %shard_map.60 = (f32[1,256,256]{2,1,0:T(8,128)S(1)}, f32[1,256,256]{2,1,0:T(8,128)S(1)}, f32[32,128]{1,0:T(8,128)S(1)}) custom-call(f32[1,5,256,256]{3,2,1,0:T(8,128)S(1)} %get-tuple-element.15.refs_0_, f32[256,256]{1,0:T(8,128)S(1)} %get-tuple-element.16.refs_1_, f32[64,64]{1,0:T(8,128)S(1)} %copy-done.2, f32[1,64,64]{2,1,0:T(8,128)S(1)} %copy-done.3, ...), custom_call_target="tpu_custom_call" | custom-call | flops 67108864 | bytes 1048576 | tf_op jit(solution)/shard_map/pallas_call | solution.py:227
  18.4 0.0 collective-permute-start.5
  18.4 1.2 %collective-permute-done.5 = f32[32,128]{1,0:T(8,128)S(1)} collective-permute-done((f32[32,128]{1,0:T(8,128)S(1)}, f32[32,128]{1,0:T(8,128)S(1)}, u32[]{:S(2)}, u32[]{:S(2)}) %collective-permute-start.5) | collective-permute-done | bytes 16416 | tf_op jit(solution)/shard_map/ppermute | solution.py:258
  19.6 2.0 %collective-permute-start.6 = (f32[32,128]{1,0:T(8,128)S(1)}, f32[32,128]{1,0:T(8,128)S(1)}, u32[]{:S(2)}, u32[]{:S(2)}) collective-permute-start(f32[32,128]{1,0:T(8,128)S(1)} %add.35), channel_id=1, source_target_pairs={{0,4},{2,6},{4,0},{6,2},{8,12},{10,14},{12,8},{14,10},{16,20},{18,... | collective-permute-start | bytes 49160 | tf_op jit(solution)/shard_map/ppermute | solution.py:258
  21.6 1.6 %collective-permute-done.3.refs_1_ = f32[256,256]{1,0:T(8,128)S(1)} collective-permute-done((f32[256,256]{1,0:T(8,128)S(1)}, f32[256,256]{1,0:T(8,128)S(1)}, u32[]{:S(2)}, u32[]{:S(2)}) %collective-permute-start.3) | collective-permute-done | bytes 262176 | tf_op jit(solution)/shard_map/ppermute | solution.py:244
  23.2 2.1 %collective-permute-start.4 = (f32[256,256]{1,0:T(8,128)S(1)}, f32[256,256]{1,0:T(8,128)S(1)}, u32[]{:S(2)}, u32[]{:S(2)}) collective-permute-start(f32[256,256]{1,0:T(8,128)S(1)} %bitcast_add_fusion.1), channel_id=1, source_target_pairs={{0,1},{1,0},{2,3},{3,2},{4,5},{5,4},{6,7},{7,6},{8,9},{9,8},{10,11... | collective-permute-start | bytes 786440 | tf_op jit(solution)/shard_map/ppermute | solution.py:244
  25.3 0.0 collective-permute-done.6
  25.3 1.6 %collective-permute-start.7 = (f32[32,128]{1,0:T(8,128)S(1)}, f32[32,128]{1,0:T(8,128)S(1)}, u32[]{:S(2)}, u32[]{:S(2)}) collective-permute-start(f32[32,128]{1,0:T(8,128)S(1)} %add.36), channel_id=1, source_target_pairs={{0,8},{2,10},{4,12},{6,14},{8,0},{10,2},{12,4},{14,6},{16,24},{18,... | collective-permute-start | bytes 49160 | tf_op jit(solution)/shard_map/ppermute | solution.py:258
  27.0 1.8 %collective-permute-done.2.refs_0_ = f32[256,256]{1,0:T(8,128)S(1)} collective-permute-done((f32[256,256]{1,0:T(8,128)S(1)}, f32[256,256]{1,0:T(8,128)S(1)}, u32[]{:S(2)}, u32[]{:S(2)}) %collective-permute-start.2) | collective-permute-done | bytes 262176 | tf_op jit(solution)/shard_map/ppermute | solution.py:244
  28.9 2.1 %collective-permute-start.10 = (f32[256,256]{1,0:T(8,128)S(1)}, f32[256,256]{1,0:T(8,128)S(1)}, u32[]{:S(2)}, u32[]{:S(2)}) collective-permute-start(f32[256,256]{1,0:T(8,128)S(1)} %bitcast_add_fusion), channel_id=1, source_target_pairs={{0,1},{1,0},{2,3},{3,2},{4,5},{5,4},{6,7},{7,6},{8,9},{9,8},{10,11... | collective-permute-start | bytes 786440 | tf_op jit(solution)/shard_map/ppermute | solution.py:244
  31.0 0.0 collective-permute-done.7
  31.0 2.6 %collective-permute-start.8 = (f32[32,128]{1,0:T(8,128)S(1)}, f32[32,128]{1,0:T(8,128)S(1)}, u32[]{:S(2)}, u32[]{:S(2)}) collective-permute-start(f32[32,128]{1,0:T(8,128)S(1)} %add.37), channel_id=1, source_target_pairs={{0,16},{2,18},{4,20},{6,22},{8,24},{10,26},{12,28},{14,30},{16,0},... | collective-permute-start | bytes 49160 | tf_op jit(solution)/shard_map/ppermute | solution.py:258
  33.6 2.1 %shard_map.61 = (f32[1,2,2,256,256]{4,3,2,1,0:T(8,128)}, f32[2,256,256]{2,1,0:T(8,128)S(1)}) custom-call(f32[2,2,256,256]{3,2,1,0:T(8,128)S(1)} %get-tuple-element.13.products, f32[256,256]{1,0:T(8,128)S(1)} %get-tuple-element.14.decay, f32[1,256,256]{2,1,0:T(8,128)S(1)} %get-tuple-element.18.alpha, f32[1,256,256]{2,1,0:T(8,128)S(1)} %get-tuple-element.19.beta, ...), custom_call_target="tpu_custom_call" | custom-call | flops 134217728 | bytes 1048576 | tf_op jit(solution)/shard_map/pallas_call | solution.py:227
  35.7 0.0 collective-permute-done.8
  35.7 0.6 %collective-permute-start.9 = (f32[32,128]{1,0:T(8,128)S(1)}, f32[32,128]{1,0:T(8,128)S(1)}, u32[]{:S(2)}, u32[]{:S(2)}) collective-permute-start(f32[32,128]{1,0:T(8,128)S(1)} %add.38.grad), channel_id=1, source_target_pairs={{0,1},{1,0},{2,3},{3,2},{4,5},{5,4},{6,7},{7,6},{8,9},{9,8},{10,11... | collective-permute-start | bytes 49160 | tf_op jit(solution)/shard_map/ppermute | solution.py:258
  36.3 0.0 collective-permute-done.4
  36.3 0.7 %bitcast_dynamic-update-slice_fusion.before = f32[1,2,2,256,256]{4,3,2,1,0:T(8,128)} fusion(f32[1,2,2,256,256]{4,3,2,1,0:T(8,128)} %get-tuple-element.21, s32[]{:T(128)S(6)} %select_n.10, f32[256,256]{1,0:T(8,128)S(1)} %collective-permute-done.4, f32[2,256,256]{2,1,0:T(8,128)S(1)} %get-tuple-element.22.refs_0_), kind=kLoop, calls=%fused_computation.1 | loop fusion | flops 131072 | bytes 786436 | tf_op jit(solution)/shard_map/dynamic_update_slice | solution.py:325
  37.1 2.5 %collective-permute-done.9.arrived = f32[32,128]{1,0:T(8,128)S(1)} collective-permute-done((f32[32,128]{1,0:T(8,128)S(1)}, f32[32,128]{1,0:T(8,128)S(1)}, u32[]{:S(2)}, u32[]{:S(2)}) %collective-permute-start.9) | collective-permute-done | bytes 16416 | tf_op jit(solution)/shard_map/ppermute | solution.py:258
  39.6 0.0 collective-permute-done.10.refs_1_
  39.6 0.7 %shard_map.62 = (f32[1,2,2,256,256]{4,3,2,1,0:T(8,128)}, f32[64,64]{1,0:T(8,128)}) custom-call(f32[1,2,2,256,256]{4,3,2,1,0:T(8,128)} %bitcast_dynamic-update-slice_fusion.before, f32[32,128]{1,0:T(8,128)S(1)} %add.38.grad, f32[32,128]{1,0:T(8,128)S(1)} %collective-permute-done.9.arrived, ...), custom_call_target="tpu_custom_call", output_to_operand_aliasing={{0}: (0, {})} | custom-call | flops 4194304 | bytes 1048576 | tf_op jit(solution)/shard_map/pallas_call | solution.py:227
  (6 shorter events, 0.1 us)
Async XLA Ops:
  0.6 8.5 %copy-start = (f32[1,2,2,256,256]{4,3,2,1,0:T(8,128)S(1)}, f32[1,2,2,256,256]{4,3,2,1,0:T(8,128)}, u32[]{:S(2)}) copy-start(f32[1,2,2,256,256]{4,3,2,1,0:T(8,128)} %state.1) | copy-start | bytes 3145732
  0.6 8.5 %copy-start.1 = (f32[1,2,2,256,256]{4,3,2,1,0:T(8,128)S(1)}, f32[1,2,2,256,256]{4,3,2,1,0:T(8,128)}, u32[]{:S(2)}) copy-start(f32[1,2,2,256,256]{4,3,2,1,0:T(8,128)} %late.1) | copy-start | bytes 3145732
  0.7 8.4 %copy-start.2 = (f32[64,64]{1,0:T(8,128)S(1)}, f32[64,64]{1,0:T(8,128)}, u32[]{:S(2)}) copy-start(f32[64,64]{1,0:T(8,128)} %refs_2_.1) | copy-start | bytes 49156
  1.8 15.8 %collective-permute-start = (f32[256,256]{1,0:T(8,128)S(1)}, f32[256,256]{1,0:T(8,128)S(1)}, u32[]{:S(2)}, u32[]{:S(2)}) collective-permute-start(f32[256,256]{1,0:T(8,128)S(1)} %dynamic-slice_bitcast_fusion.3), channel_id=1, source_target_pairs={{0,1},{1,0},{2,3},{3,2},{4,5},{5,4},{6,7},{7,6},{8,9},{9,8},{10,11... | collective-permute-start | bytes 786440 | tf_op jit(solution)/shard_map/ppermute | solution.py:244
  5.8 11.8 %collective-permute-start.1 = (f32[256,256]{1,0:T(8,128)S(1)}, f32[256,256]{1,0:T(8,128)S(1)}, u32[]{:S(2)}, u32[]{:S(2)}) collective-permute-start(f32[256,256]{1,0:T(8,128)S(1)} %dynamic-slice_bitcast_fusion.2.refs_6_), channel_id=1, source_target_pairs={{0,1},{1,0},{2,3},{3,2},{4,5},{5,4},{6,7},{7,6},{8,9},{9,8},{10,11... | collective-permute-start | bytes 786440 | tf_op jit(solution)/shard_map/ppermute | solution.py:244
  6.9 16.3 %collective-permute-start.3 = (f32[256,256]{1,0:T(8,128)S(1)}, f32[256,256]{1,0:T(8,128)S(1)}, u32[]{:S(2)}, u32[]{:S(2)}) collective-permute-start(f32[256,256]{1,0:T(8,128)S(1)} %get-tuple-element.25.refs_7_), channel_id=1, source_target_pairs={{0,1},{1,0},{2,3},{3,2},{4,5},{5,4},{6,7},{7,6},{8,9},{9,8},{10,11... | collective-permute-start | bytes 786440 | tf_op jit(solution)/shard_map/ppermute | solution.py:244
  9.0 19.8 %collective-permute-start.2 = (f32[256,256]{1,0:T(8,128)S(1)}, f32[256,256]{1,0:T(8,128)S(1)}, u32[]{:S(2)}, u32[]{:S(2)}) collective-permute-start(f32[256,256]{1,0:T(8,128)S(1)} %get-tuple-element.24), channel_id=1, source_target_pairs={{0,1},{1,0},{2,3},{3,2},{4,5},{5,4},{6,7},{7,6},{8,9},{9,8},{10,11... | collective-permute-start | bytes 786440 | tf_op jit(solution)/shard_map/ppermute | solution.py:244
  9.1 0.8 %copy-start.3 = (f32[1,64,64]{2,1,0:T(8,128)S(1)}, f32[1,64,64]{2,1,0:T(8,128)}, u32[]{:S(2)}) copy-start(f32[1,64,64]{2,1,0:T(8,128)} %refs_3_.1) | copy-start | bytes 49156
  18.4 1.2 %collective-permute-start.5 = (f32[32,128]{1,0:T(8,128)S(1)}, f32[32,128]{1,0:T(8,128)S(1)}, u32[]{:S(2)}, u32[]{:S(2)}) collective-permute-start(f32[32,128]{1,0:T(8,128)S(1)} %get-tuple-element.23), channel_id=1, source_target_pairs={{0,2},{2,0},{4,6},{6,4},{8,10},{10,8},{12,14},{14,12},{16,18},{18,... | collective-permute-start | bytes 49160 | tf_op jit(solution)/shard_map/ppermute | solution.py:258
  19.6 5.8 %collective-permute-start.6 = (f32[32,128]{1,0:T(8,128)S(1)}, f32[32,128]{1,0:T(8,128)S(1)}, u32[]{:S(2)}, u32[]{:S(2)}) collective-permute-start(f32[32,128]{1,0:T(8,128)S(1)} %add.35), channel_id=1, source_target_pairs={{0,4},{2,6},{4,0},{6,2},{8,12},{10,14},{12,8},{14,10},{16,20},{18,... | collective-permute-start | bytes 49160 | tf_op jit(solution)/shard_map/ppermute | solution.py:258
  23.2 13.1 %collective-permute-start.4 = (f32[256,256]{1,0:T(8,128)S(1)}, f32[256,256]{1,0:T(8,128)S(1)}, u32[]{:S(2)}, u32[]{:S(2)}) collective-permute-start(f32[256,256]{1,0:T(8,128)S(1)} %bitcast_add_fusion.1), channel_id=1, source_target_pairs={{0,1},{1,0},{2,3},{3,2},{4,5},{5,4},{6,7},{7,6},{8,9},{9,8},{10,11... | collective-permute-start | bytes 786440 | tf_op jit(solution)/shard_map/ppermute | solution.py:244
  25.3 5.6 %collective-permute-start.7 = (f32[32,128]{1,0:T(8,128)S(1)}, f32[32,128]{1,0:T(8,128)S(1)}, u32[]{:S(2)}, u32[]{:S(2)}) collective-permute-start(f32[32,128]{1,0:T(8,128)S(1)} %add.36), channel_id=1, source_target_pairs={{0,8},{2,10},{4,12},{6,14},{8,0},{10,2},{12,4},{14,6},{16,24},{18,... | collective-permute-start | bytes 49160 | tf_op jit(solution)/shard_map/ppermute | solution.py:258
  28.9 10.7 %collective-permute-start.10 = (f32[256,256]{1,0:T(8,128)S(1)}, f32[256,256]{1,0:T(8,128)S(1)}, u32[]{:S(2)}, u32[]{:S(2)}) collective-permute-start(f32[256,256]{1,0:T(8,128)S(1)} %bitcast_add_fusion), channel_id=1, source_target_pairs={{0,1},{1,0},{2,3},{3,2},{4,5},{5,4},{6,7},{7,6},{8,9},{9,8},{10,11... | collective-permute-start | bytes 786440 | tf_op jit(solution)/shard_map/ppermute | solution.py:244
  31.0 4.7 %collective-permute-start.8 = (f32[32,128]{1,0:T(8,128)S(1)}, f32[32,128]{1,0:T(8,128)S(1)}, u32[]{:S(2)}, u32[]{:S(2)}) collective-permute-start(f32[32,128]{1,0:T(8,128)S(1)} %add.37), channel_id=1, source_target_pairs={{0,16},{2,18},{4,20},{6,22},{8,24},{10,26},{12,28},{14,30},{16,0},... | collective-permute-start | bytes 49160 | tf_op jit(solution)/shard_map/ppermute | solution.py:258
  35.7 3.9 %collective-permute-start.9 = (f32[32,128]{1,0:T(8,128)S(1)}, f32[32,128]{1,0:T(8,128)S(1)}, u32[]{:S(2)}, u32[]{:S(2)}) collective-permute-start(f32[32,128]{1,0:T(8,128)S(1)} %add.38.grad), channel_id=1, source_target_pairs={{0,1},{1,0},{2,3},{3,2},{4,5},{5,4},{6,7},{7,6},{8,9},{9,8},{10,11... | collective-permute-start | bytes 49160 | tf_op jit(solution)/shard_map/ppermute | solution.py:258
